TPU v7x, 32 devices: a whole 2x2x4 slice. The times are simulated.
32 devices in a mesh: ty: 4 (over z), tx: 8 (over y, x, core).
Axes of the slice: x: 2, y: 2, z: 4, core: 2. Of those that a mesh axis runs over, the one named last changes fastest.
Arguments:
- object_slices: float32 [2, 2, 2048, 4096], P(None, None, 'ty', 'tx'), may hold values from -4 to 4
- probe_modes: float32 [4, 2, 128, 128], replicated, may hold values from -12 to 12
- patterns: bfloat16 [256, 128, 128], P(('ty', 'tx')), may hold values from 0 to 2
- positions: int32 [256, 2], replicated, may hold values from 0 to 4095, as said below
- counts: int32 [32], replicated, may hold values from 6 to 8, as said below
Outputs:
- new_object: float32 [2, 2, 2048, 4096], P(None, None, 'ty', 'tx')
- new_probe: float32 [4, 2, 128, 128], replicated
Inputs may be any that keep to these rules, and one draw needn't show every extreme that they name: positions[j] is the centre of pattern j, which was acquired by device j // 8 of ty+tx (ty slowest); its column lies in that device's column of tiles of 512 x 512 cells. Of the live patterns of one device, at most 2 lie in any one row of tiles; in every column of tiles some row of tiles holds exactly 2 live patterns from every device of that column. The live patterns of device d are its first counts[d] slots; some device has 8.
All inputs are finite; a program needn't handle non-finite values.
Results may differ from a plain program's by a relative error of at most 0.0085.
The roundings to bfloat16 on the way count: a program that leaves them out, or rounds other values in their place, can miss the bound.
Values may be sent and summed in bfloat16 or wider, within the bound.
No kernel may reach another device: no remote copies, remote signals or barrier semaphores. Data moves between devices by JAX's collectives and lax.ppermute only.
A program may use at most 128 MiB of HBM per device.

v0:
```python
import math
import jax
import jax.numpy as jnp
from jax import lax
from jax.sharding import PartitionSpec as P

CAP = 2
PROPAGATION = 0.37


def extended_2(block, sides, width):
    for axis, dim in sides:
        count = lax.axis_size(axis)
        forward = [(i, i + 1) for i in range(count - 1)]
        backward = [(target, source) for source, target in forward]
        low = lax.ppermute(
            lax.slice_in_dim(block, block.shape[dim] - width, None, axis=dim), axis, forward
        )
        high = lax.ppermute(lax.slice_in_dim(block, 0, width, axis=dim), axis, backward)
        block = jnp.concatenate([low, block, high], axis=dim)
    return block


def make_tables(extent):
    indices = jnp.arange(extent, dtype=jnp.int32)
    product = indices[:, None] * indices[None, :] % extent
    angles = 2.0 * jnp.pi / extent * product.astype(jnp.float32)
    norm_scale = 1.0 / math.sqrt(extent)
    real_table = (jnp.cos(angles) * norm_scale).astype(jnp.bfloat16)
    imag_table = (-jnp.sin(angles) * norm_scale).astype(jnp.bfloat16)
    right_fwd = jnp.concatenate(
        [
            jnp.concatenate([real_table, imag_table], 1),
            jnp.concatenate([-imag_table, real_table], 1),
        ],
        0,
    )
    right_inv = jnp.concatenate(
        [
            jnp.concatenate([real_table, -imag_table], 1),
            jnp.concatenate([imag_table, real_table], 1),
        ],
        0,
    )
    left_fwd = jnp.concatenate([real_table, imag_table], 0)
    left_inv = jnp.concatenate([real_table, -imag_table], 0)
    frequency = jnp.where(indices < extent // 2, indices, indices - extent).astype(jnp.float32)
    phases = -jnp.pi * PROPAGATION / extent * (frequency[:, None] ** 2 + frequency[None, :] ** 2)
    kernel = jnp.stack([jnp.cos(phases), jnp.sin(phases)])
    return (right_fwd, left_fwd, right_inv, left_inv, kernel)


def transform(wave_field, right_table, left_table):
    extent = wave_field.shape[-1]
    rounded = wave_field.astype(jnp.bfloat16)
    joined = jnp.concatenate([rounded[:, 0], rounded[:, 1]], axis=-1)
    partial_value = jnp.einsum(
        "bpk,kq->bpq", joined, right_table, preferred_element_type=jnp.float32
    ).astype(jnp.bfloat16)
    stacked = jnp.einsum(
        "ij,bjq->biq", left_table, partial_value, preferred_element_type=jnp.float32
    )
    real_part = stacked[:, :extent, :extent] - stacked[:, extent:, extent:]
    imag_part = stacked[:, extent:, :extent] + stacked[:, :extent, extent:]
    return jnp.stack([real_part, imag_part], axis=1)


def complex_product(former, latter):
    former_re = former[..., 0, :, :]
    former_im = former[..., 1, :, :]
    latter_re = latter[..., 0, :, :]
    latter_im = latter[..., 1, :, :]
    return jnp.stack(
        [
            former_re * latter_re - former_im * latter_im,
            former_re * latter_im + former_im * latter_re,
        ],
        axis=-3,
    )


def conjugate(values):
    return jnp.stack([values[..., 0, :, :], -values[..., 1, :, :]], axis=-3)


def pattern_terms(window, amplitude, live_flag, probe_modes, tables):
    right_fwd, left_fwd, right_inv, left_inv, kernel = tables
    slices = window.shape[0]
    inputs = [probe_modes]
    far_field = None
    for slice_index in range(slices):
        exit_wave = complex_product(inputs[slice_index], window[slice_index])
        if slice_index + 1 < slices:
            spread_wave = complex_product(kernel, transform(exit_wave, right_fwd, left_fwd))
            inputs.append(transform(spread_wave, right_inv, left_inv))
        else:
            far_field = transform(exit_wave, right_fwd, left_fwd)
    intensity = jnp.sum(far_field[:, 0] ** 2 + far_field[:, 1] ** 2, axis=0)
    factor = (1.0 - amplitude / jnp.sqrt(jnp.maximum(intensity, 0.25))) * live_flag
    residue = far_field * factor
    backward = transform(residue, right_inv, left_inv)
    slice_grads = [None] * slices
    for slice_index in reversed(range(slices)):
        slice_grads[slice_index] = jnp.sum(
            complex_product(conjugate(inputs[slice_index]), backward), axis=0
        )
        if slice_index > 0:
            inner_wave = transform(
                complex_product(conjugate(window[slice_index]), backward), right_fwd, left_fwd
            )
            backward = transform(
                complex_product(conjugate(kernel), inner_wave), right_inv, left_inv
            )
    probe_term = complex_product(conjugate(window[0]), backward)
    return (jnp.stack(slice_grads), probe_term)


def settle(centre, leading, trailing, axis, margin):
    length = centre.shape[axis]
    top_part = lax.slice_in_dim(centre, 0, margin, axis=axis) + leading
    middle_part = lax.slice_in_dim(centre, margin, length - margin, axis=axis)
    bottom_part = lax.slice_in_dim(centre, length - margin, length, axis=axis) + trailing
    return jnp.concatenate([top_part, middle_part, bottom_part], axis=axis)


def on_device(object_slices, probe_modes, patterns, positions, counts):
    slices = object_slices.shape[0]
    tile_cells = object_slices.shape[2]
    extent = probe_modes.shape[-1]
    margin = extent // 2
    per_device = patterns.shape[0]
    row_count = lax.axis_size("ty")
    column_count = lax.axis_size("tx")
    row_index = lax.axis_index("ty")
    column_index = lax.axis_index("tx")
    position_grid = positions.reshape(row_count, column_count, per_device, 2)
    column = lax.dynamic_index_in_dim(position_grid, column_index, axis=1, keepdims=False)
    count_grid = counts.reshape(row_count, column_count)
    column_counts = lax.dynamic_index_in_dim(count_grid, column_index, axis=1, keepdims=False)
    ordinal = jnp.arange(per_device, dtype=jnp.int32)
    is_live = ordinal[None, :] < column_counts[:, None]
    target = column[:, :, 0] // tile_cells
    earlier = ordinal[None, :] < ordinal[:, None]
    same_row = is_live[:, None, :] & (target[:, None, :] == target[:, :, None]) & earlier[None]
    row_rank = jnp.sum(same_row.astype(jnp.int32), axis=2)
    slot_count = row_count * CAP
    slot_ids = jnp.arange(slot_count, dtype=jnp.int32)
    own_live = lax.dynamic_index_in_dim(is_live, row_index, axis=0, keepdims=False)
    own_slot = lax.dynamic_index_in_dim(target * CAP + row_rank, row_index, axis=0, keepdims=False)
    choose = (own_live[None, :] & (own_slot[None, :] == slot_ids[:, None])).astype(jnp.bfloat16)
    outgoing = jnp.einsum(
        "sj,jab->sab", choose, patterns, preferred_element_type=jnp.float32
    ).astype(jnp.bfloat16)
    incoming = lax.all_to_all(outgoing, "ty", split_axis=0, concat_axis=0, tiled=True)
    rank_ids = jnp.arange(CAP, dtype=jnp.int32)
    matched = (
        is_live[:, None, :]
        & (target[:, None, :] == row_index)
        & (row_rank[:, None, :] == rank_ids[None, :, None])
    )
    slot_live = jnp.any(matched, axis=2).reshape(-1)
    chosen = matched.astype(jnp.int32)
    centre_row = jnp.sum(chosen * column[:, None, :, 0], axis=2).reshape(-1)
    centre_col = jnp.sum(chosen * column[:, None, :, 1], axis=2).reshape(-1)
    local_row = jnp.where(slot_live, centre_row - row_index * tile_cells, 0)
    local_col = jnp.where(slot_live, centre_col - column_index * tile_cells, 0)
    extended = extended_2(object_slices, (("ty", 2), ("tx", 3)), margin)
    tables = make_tables(extent)

    def visit_slot(running, element):
        gradient, probe_grad = running
        amplitude, row_start, col_start, live_flag = element
        corner = (jnp.int32(0), jnp.int32(0), row_start, col_start)
        window = lax.dynamic_slice(extended, corner, (slices, 2, extent, extent))
        slice_grads, probe_term = pattern_terms(
            window, amplitude.astype(jnp.float32), live_flag, probe_modes, tables
        )
        current = lax.dynamic_slice(gradient, corner, (slices, 2, extent, extent))
        gradient = lax.dynamic_update_slice(gradient, current + slice_grads, corner)
        return ((gradient, probe_grad + probe_term), None)

    span_cells = tile_cells + extent
    initial = (
        jnp.zeros((slices, 2, span_cells, span_cells), jnp.float32),
        jnp.zeros(probe_modes.shape, jnp.float32),
    )
    (gradient, probe_grad), unused = lax.scan(
        visit_slot, initial, (incoming, local_row, local_col, slot_live.astype(jnp.float32))
    )
    row_edges = jnp.concatenate([gradient[:, :, :margin], gradient[:, :, -margin:]], axis=2)
    row_halo = extended_2(row_edges, (("ty", 2),), margin)
    row_folded = settle(
        gradient[:, :, margin : margin + tile_cells],
        row_halo[:, :, :margin],
        row_halo[:, :, -margin:],
        2,
        margin,
    )
    col_edges = jnp.concatenate([row_folded[..., :margin], row_folded[..., -margin:]], axis=3)
    col_halo = extended_2(col_edges, (("tx", 3),), margin)
    folded = settle(
        row_folded[..., margin : margin + tile_cells],
        col_halo[..., :margin],
        col_halo[..., -margin:],
        3,
        margin,
    )
    probe_power = jnp.mean(jnp.sum(probe_modes**2, axis=(0, 1)))
    new_object = object_slices - folded / (probe_power + 1e-06)
    summed = lax.psum(probe_grad, ("ty", "tx"))
    spread = jnp.sqrt(jnp.mean(summed * summed) + 1e-06)
    new_probe = probe_modes - 0.5 * summed / spread
    return (new_object, new_probe)


def solution(mesh):
    return jax.shard_map(
        on_device,
        mesh=mesh,
        in_specs=(P(None, None, "ty", "tx"), P(), P(("ty", "tx"), None, None), P(), P()),
        out_specs=(P(None, None, "ty", "tx"), P()),
        check_vma=False,
    )
```

profile of v0, /device:TPU:0, one launch (start us, length us, event | category | flops | bytes accessed | tf_op | source)
XLA Modules:
  0.0 498.1 jit_solution(16212770416473145393)
XLA Ops:
  10.3 6.3 %all-to-all-start = ((bf16[8,128,128]{2,1,0:T(8,128)(2,1)}), bf16[8,128,128]{2,1,0:T(8,128)(2,1)}, u32[]{:S(2)}, u32[]{:S(2)}) async-start(bf16[8,128,128]{2,1,0:T(8,128)(2,1)} %copy.108), calls=%async_computation | async-start | bytes 524288 | tf_op jit(solution)/shard_map/all_to_all | solution.py:154
  18.0 4.0 collective-permute-start
  23.2 5.2 %copy.120 = f32[2,2,512,512]{2,3,1,0:T(8,128)} copy(f32[2,2,512,512]{3,2,1,0:T(8,128)} %param.7) | data formatting | bytes 8388608 | tf_op args[0]
  30.5 2.0 collective-permute-done
  32.8 4.0 collective-permute-done.1
  37.2 2.8 pad_maximum_fusion.4
  40.0 2.1 collective-permute-start.2
  47.4 5.9 %pad_maximum_fusion = f32[2,2,640,640]{2,3,1,0:T(8,128)} fusion(f32[2,2,640,64]{2,3,1,0:T(8,128)} %collective-permute-done.3, f32[2,2,64,512]{2,3,1,0:T(8,128)S(1)} %copy.106, f32[2,2,512,512]{2,3,1,0:T(8,128)} %copy.120, f32[2,2,64,512]{2,3,1,0:T(8,128)S(1)} %copy.104, f32[2,2,640,64]{2,3,1,0:T(8,128)} %collective-permute-done.2), kind=kLoop, calls=%fused_computation.110 | loop fusion | flops 6553600 | bytes 13107200 | tf_op jit(solution)/shard_map/concatenate | solution.py:20
  53.3 3.2 broadcast_in_dim.8
  56.5 217.4 %while.18 = (s32[]{:T(128)}, f32[2,2,640,640]{2,3,1,0:T(8,128)}, f32[4,2,128,128]{3,2,0,1:T(8,128)S(1)}, s32[8]{0:T(128)S(1)}, s32[8]{0:T(128)S(1)}, /*index=5*/...) while((s32[]{:T(128)}, f32[2,2,640,640]{2,3,1,0:T(8,128)}, ...), condition=%wide.region_8.9_spmd.clone.clone.clone.clone, body=%wide.region_4.8_spmd.clone.clone.clone.clone.sunk | while | flops 815677440 | bytes 33391468 | solution.py:187
  79.3 4.4 dynamic_update_slice.10
  106.5 4.2 dynamic_update_slice.10
  133.5 4.4 dynamic_update_slice.10
  160.7 4.4 dynamic_update_slice.10
  187.9 4.4 dynamic_update_slice.10
  215.1 4.3 dynamic_update_slice.10
  242.2 4.4 dynamic_update_slice.10
  269.4 4.4 dynamic_update_slice.10
  273.8 8.2 %copy.114 = f32[2,2,640,640]{3,2,1,0:T(8,128)} copy(f32[2,2,640,640]{2,3,1,0:T(8,128)} %get-tuple-element.206) | data formatting | bytes 13107200 | tf_op jit(solution)/shard_map/while | solution.py:187
  285.0 8.0 %collective-permute-done.4 = f32[2,2,64,640]{3,2,1,0:T(8,128)S(1)} collective-permute-done((f32[2,2,64,640]{3,2,1,0:T(8,128)S(1)}, f32[2,2,64,640]{3,2,1,0:T(8,128)S(1)}, u32[]{:S(2)}, u32[]{:S(2)}) %collective-permute-start.4) | collective-permute-done | bytes 655392 | tf_op jit(solution)/shard_map/ppermute | solution.py:16
  293.1 2.3 slice_add_fusion.7
  296.8 4.2 slice.281
  301.4 7.1 %collective-permute-done.5 = f32[2,2,64,640]{3,2,1,0:T(8,128)S(1)} collective-permute-done((f32[2,2,64,640]{3,2,1,0:T(8,128)}, f32[2,2,64,640]{3,2,1,0:T(8,128)S(1)}, u32[]{:S(2)}, u32[]{:S(2)}) %collective-permute-start.5) | collective-permute-done | bytes 655392 | tf_op jit(solution)/shard_map/ppermute | solution.py:19
  308.5 2.0 slice_add_fusion.6
  312.0 2.0 pad_maximum_fusion.6
  314.0 14.0 %collective-permute-start.6 = (f32[2,2,512,64]{2,3,1,0:T(8,128)}, f32[2,2,512,64]{2,3,1,0:T(8,128)}, u32[]{:S(2)}, u32[]{:S(2)}) collective-permute-start(f32[2,2,512,64]{2,3,1,0:T(8,128)} %pad_maximum_fusion.6), channel_id=1, source_target_pairs={{0,1},{1,2},{2,3},{3,4},{4,5},{5,6},{6,7},{8,9},{9,10},{10,11},{11... | collective-permute-start | bytes 1572872 | tf_op jit(solution)/shard_map/ppermute | solution.py:16
  329.1 2.7 maximum_add_fusion.3
  333.0 136.7 %all-reduce.2.cloned.1.call-done = f32[4,2,128,128]{3,2,1,0:T(8,128)} async-done(((f32[4,2,128,128]{3,2,1,0:T(8,128)}), f32[4,2,128,128]{3,2,1,0:T(8,128)}) %all-reduce.2.cloned.1.call-update) | async-done | bytes 524304 | tf_op jit(solution)/shard_map/psum | solution.py:210
  472.2 2.5 divide_subtract_fusion
  475.4 3.9 pad_maximum_fusion.1
  483.1 3.0 fusion.85
  486.1 5.2 %copy.122 = f32[2,2,512,512]{3,2,1,0:T(8,128)} copy(f32[2,2,512,512]{2,3,1,0:T(8,128)} %fusion.85) | data formatting | bytes 8388608
  (387 shorter events, 177.5 us)
Async XLA Ops:
  7.2 2.1 copy-start
  10.3 43.0 %all-to-all-start = ((bf16[8,128,128]{2,1,0:T(8,128)(2,1)}), bf16[8,128,128]{2,1,0:T(8,128)(2,1)}, u32[]{:S(2)}, u32[]{:S(2)}) async-start(bf16[8,128,128]{2,1,0:T(8,128)(2,1)} %copy.108), calls=%async_computation | async-start | bytes 524288 | tf_op jit(solution)/shard_map/all_to_all | solution.py:154
  16.7 453.1 %all-reduce.2.cloned.1.call-start = ((), (), s32[]{:S(2)}) async-start(), calls=%async_computation.1 | async-start | bytes 1048576 | tf_op jit(solution)/shard_map/psum | solution.py:210
  18.0 14.5 %collective-permute-start = (f32[2,2,64,512]{3,2,1,0:T(8,128)S(1)}, f32[2,2,64,512]{3,2,1,0:T(8,128)S(1)}, u32[]{:S(2)}, u32[]{:S(2)}) collective-permute-start(f32[2,2,64,512]{3,2,1,0:T(8,128)S(1)} %get-tuple-element.545), channel_id=1, source_target_pairs={{0,8},{8,16},{16,24},{1,9},{9,17},{17,25},{2,10},{10,18},{18,26},{... | collective-permute-start | bytes 1572872 | tf_op jit(solution)/shard_map/ppermute | solution.py:16
  21.9 14.9 %collective-permute-start.1 = (f32[2,2,64,512]{3,2,1,0:T(8,128)S(1)}, f32[2,2,64,512]{3,2,1,0:T(8,128)S(1)}, u32[]{:S(2)}, u32[]{:S(2)}) collective-permute-start(f32[2,2,64,512]{3,2,1,0:T(8,128)S(1)} %get-tuple-element.546), channel_id=1, source_target_pairs={{8,0},{16,8},{24,16},{9,1},{17,9},{25,17},{10,2},{18,10},{26,18},{... | collective-permute-start | bytes 1572872 | tf_op jit(solution)/shard_map/ppermute | solution.py:19
  29.8 0.6 copy-start.10
  29.9 0.6 copy-start.12
  37.1 6.3 %copy-start.9 = (bf16[128,128]{1,0:T(8,128)(2,1)S(1)}, bf16[128,128]{1,0:T(8,128)(2,1)}, u32[]{:S(2)}) copy-start(bf16[128,128]{1,0:T(8,128)(2,1)} %copy-done.8) | copy-start | bytes 98308
  37.2 6.3 %copy-start.11 = (bf16[128,128]{1,0:T(8,128)(2,1)S(1)}, bf16[128,128]{1,0:T(8,128)(2,1)}, u32[]{:S(2)}) copy-start(bf16[128,128]{1,0:T(8,128)(2,1)} %copy-done.10) | copy-start | bytes 98308
  37.2 6.3 %copy-start.13 = (bf16[128,128]{1,0:T(8,128)(2,1)S(1)}, bf16[128,128]{1,0:T(8,128)(2,1)}, u32[]{:S(2)}) copy-start(bf16[128,128]{1,0:T(8,128)(2,1)} %copy-done.12) | copy-start | bytes 98308
  37.2 6.3 %copy-start.14 = (pred[4,2]{0,1:T(4,128)(4,1)S(1)}, pred[4,2]{0,1:T(4,128)(4,1)}, u32[]{:S(2)}) copy-start(pred[4,2]{0,1:T(4,128)(4,1)} %reduce_or.9) | copy-start | bytes 28
  37.2 6.3 %copy-start.5 = (f32[4,2,128,128]{3,2,1,0:T(8,128)S(1)}, f32[4,2,128,128]{3,2,1,0:T(8,128)}, u32[]{:S(2)}) copy-start(f32[4,2,128,128]{3,2,1,0:T(8,128)} %param.8) | copy-start | bytes 1572868
  40.0 6.6 %collective-permute-start.2 = (f32[2,2,640,64]{2,3,1,0:T(8,128)}, f32[2,2,640,64]{2,3,1,0:T(8,128)}, u32[]{:S(2)}, u32[]{:S(2)}) collective-permute-start(f32[2,2,640,64]{2,3,1,0:T(8,128)} %get-tuple-element.543), channel_id=1, source_target_pairs={{0,1},{1,2},{2,3},{3,4},{4,5},{5,6},{6,7},{8,9},{9,10},{10,11},{11... | collective-permute-start | bytes 1966088 | tf_op jit(solution)/shard_map/ppermute | solution.py:16
  42.1 5.2 %collective-permute-start.3 = (f32[2,2,640,64]{2,3,1,0:T(8,128)}, f32[2,2,640,64]{2,3,1,0:T(8,128)}, u32[]{:S(2)}, u32[]{:S(2)}) collective-permute-start(f32[2,2,640,64]{2,3,1,0:T(8,128)} %get-tuple-element.544), channel_id=1, source_target_pairs={{1,0},{2,1},{3,2},{4,3},{5,4},{6,5},{7,6},{9,8},{10,9},{11,10},{12... | collective-permute-start | bytes 1966088 | tf_op jit(solution)/shard_map/ppermute | solution.py:19
  53.3 3.2 copy-start.15
  75.3 2.3 copy-start.4
  102.5 2.3 copy-start.4
  129.5 2.3 copy-start.4
  156.7 2.3 copy-start.4
  183.9 2.3 copy-start.4
  211.1 2.3 copy-start.4
  238.2 2.3 copy-start.4
  265.5 2.3 copy-start.4
  283.1 9.9 %collective-permute-start.4 = (f32[2,2,64,640]{3,2,1,0:T(8,128)S(1)}, f32[2,2,64,640]{3,2,1,0:T(8,128)S(1)}, u32[]{:S(2)}, u32[]{:S(2)}) collective-permute-start(f32[2,2,64,640]{3,2,1,0:T(8,128)S(1)} %slice.455), channel_id=1, source_target_pairs={{0,8},{8,16},{16,24},{1,9},{9,17},{17,25},{2,10},{10,18},{18,26},{... | collective-permute-start | bytes 1966088 | tf_op jit(solution)/shard_map/ppermute | solution.py:16
  295.3 13.1 %collective-permute-start.5 = (f32[2,2,64,640]{3,2,1,0:T(8,128)}, f32[2,2,64,640]{3,2,1,0:T(8,128)S(1)}, u32[]{:S(2)}, u32[]{:S(2)}) collective-permute-start(f32[2,2,64,640]{3,2,1,0:T(8,128)} %get-tuple-element.542), channel_id=1, source_target_pairs={{8,0},{16,8},{24,16},{9,1},{17,9},{25,17},{10,2},{18,10},{26,18},{... | collective-permute-start | bytes 1966088 | tf_op jit(solution)/shard_map/ppermute | solution.py:19
  314.0 15.1 %collective-permute-start.6 = (f32[2,2,512,64]{2,3,1,0:T(8,128)}, f32[2,2,512,64]{2,3,1,0:T(8,128)}, u32[]{:S(2)}, u32[]{:S(2)}) collective-permute-start(f32[2,2,512,64]{2,3,1,0:T(8,128)} %pad_maximum_fusion.6), channel_id=1, source_target_pairs={{0,1},{1,2},{2,3},{3,4},{4,5},{5,6},{6,7},{8,9},{9,10},{10,11},{11... | collective-permute-start | bytes 1572872 | tf_op jit(solution)/shard_map/ppermute | solution.py:16
  328.9 143.3 %copy-start.6 = (f32[4,2,128,128]{3,2,1,0:T(8,128)S(1)}, f32[4,2,128,128]{3,2,1,0:T(8,128)}, u32[]{:S(2)}) copy-start(f32[4,2,128,128]{3,2,1,0:T(8,128)} %param.8) | copy-start | bytes 1572868
  331.7 147.9 %collective-permute-start.7 = (f32[2,2,512,64]{2,3,1,0:T(8,128)}, f32[2,2,512,64]{2,3,1,0:T(8,128)}, u32[]{:S(2)}, u32[]{:S(2)}) collective-permute-start(f32[2,2,512,64]{2,3,1,0:T(8,128)} %get-tuple-element.540), channel_id=1, source_target_pairs={{1,0},{2,1},{3,2},{4,3},{5,4},{6,5},{7,6},{9,8},{10,9},{11,10},{12... | collective-permute-start | bytes 1572872 | tf_op jit(solution)/shard_map/ppermute | solution.py:19
  479.3 2.1 copy-start.2
  479.6 3.5 copy-start.3
  479.6 3.5 copy-start.7
  483.1 8.2 %copy-start.1 = (bf16[8,128,128]{2,1,0:T(8,128)(2,1)S(1)}, bf16[8,128,128]{2,1,0:T(8,128)(2,1)}, u32[]{:S(2)}) copy-start(bf16[8,128,128]{2,1,0:T(8,128)(2,1)} %param.9) | copy-start | bytes 786436
  (1 other events, 0.6 us)
Sparse Core Ops, SparseCore 0:
  329.0 140.7 all-reduce.1
where the time goes:
time: 503 us; the launch traced here: 498 us
  waiting for transfers between devices  159 us (32%)
  local copies, waits for them, and re-layouts  119 us (24%)
  other arithmetic  88.5 us (18%)
  matrix products  49.7 us (10%)
  starting transfers between devices  33.7 us (7%)
  loops' own time  32.6 us (6%)
  between operations  15.8 us (3%)
    psum x1, waiting for transfers between devices, on_device(): summed = lax.psum(probe_grad, ('ty', 'tx'))  137 us
    dot_general x48, matrix products, transform(): jnp.einsum('ij,bjq->biq', left_table, partial_value, preferred_element_ty...  49.5 us
    dynamic_update_slice x8, local copies, waits for them, and re-layouts, visit_slot(): gradient = lax.dynamic_update_slice(gradient, current + slice_grads, corner)  34.9 us
    another operation x1, loops' own time, on_device(): lax.scan(visit_slot, initial, (incoming, local_row, local_col, slot_live....  32.6 us
    dynamic_slice x40, local copies, waits for them, and re-layouts, on_device(): lax.scan(visit_slot, initial, (incoming, local_row, local_col, slot_live....  26.4 us
    ppermute x4, starting transfers between devices, extended_2(): lax.ppermute(lax.slice_in_dim(block, block.shape[dim] - width, None, axis...  22 us
    squeeze x48, other arithmetic, transform(): joined = jnp.concatenate([rounded[:, 0], rounded[:, 1]], axis=-1)  20.9 us
    unnamed x33, local copies, waits for them, and re-layouts  12.9 us
  transfers between devices with their start and end apart: 10, of which 7 were waited for; matrix products, arithmetic and copies ran while one was open for 7% of the time, Pallas kernels for 0%

commit v1 on v0

--- a/solution.py
+++ b/solution.py
@@ -207,7 +207,7 @@
     )
     probe_power = jnp.mean(jnp.sum(probe_modes**2, axis=(0, 1)))
     new_object = object_slices - folded / (probe_power + 1e-06)
-    summed = lax.psum(probe_grad, ("ty", "tx"))
+    summed = jnp.sum(lax.all_gather(probe_grad, ("ty", "tx")), axis=0)
     spread = jnp.sqrt(jnp.mean(summed * summed) + 1e-06)
     new_probe = probe_modes - 0.5 * summed / spread
     return (new_object, new_probe)

time: 503 us -> 464 us (0.922)
  waiting for transfers between devices: 159 us -> 96.8 us
  other arithmetic: 88.5 us -> 104 us
  starting transfers between devices: 33.7 us -> 40.1 us
  local copies, waits for them, and re-layouts: 119 us -> 113 us
  matrix products: 49.7 us -> 55.2 us
    psum x1 -> x0, waiting for transfers between devices: 137 us -> none  [on_device(): summed = lax.psum(probe_grad, ('ty', 'tx'))]
    ppermute x4, waiting for transfers between devices: 11.7 us -> 57.6 us  [extended_2(): lax.ppermute(lax.slice_in_dim(block, 0, width, axis=dim), axis, backward)]
    all_gather x0 -> x1, waiting for transfers between devices: none -> 29.7 us  [on_device(): summed = jnp.sum(lax.all_gather(probe_grad, ('ty', 'tx')), axis=0)]
    another operation x24, other arithmetic: 2.18 us -> 16.5 us  [complex_product(): jnp.stack([former_re * latter_re - former_im * latter_im, former_re * lat...]
    squeeze x48, other arithmetic: 20.9 us -> 10.3 us  [transform(): joined = jnp.concatenate([rounded[:, 0], rounded[:, 1]], axis=-1)]
    ppermute x4, starting transfers between devices: 22 us -> 30.5 us  [extended_2(): lax.ppermute(lax.slice_in_dim(block, block.shape[dim] - width, None, axis...]
    reduce_sum x0 -> x2, other arithmetic: none -> 7.68 us  [the longest x1 6.98 us: on_device(): summed = jnp.sum(lax.all_gather(probe_grad, ('ty', 'tx')), axis=0)]
    neg x17, other arithmetic: 0.84 us -> 7.54 us  [conjugate(): return jnp.stack([values[..., 0, :, :], -values[..., 1, :, :]], axis=-3)]
  transfers between devices with their start and end apart: 10 -> 10, of which waited for: 7 -> 5; matrix products, arithmetic and copies ran while one was open for 7% -> 12% of each run, Pallas kernels for 0% -> 0%
where the time goes in v1:
time: 464 us; the launch traced here: 458 us
  local copies, waits for them, and re-layouts  113 us (24%)
  other arithmetic  104 us (22%)
  waiting for transfers between devices  96.8 us (21%)
  matrix products  55.2 us (12%)
  starting transfers between devices  40.1 us (9%)
  loops' own time  33.2 us (7%)
  between operations  15.7 us (3%)
    ppermute x4, waiting for transfers between devices, extended_2(): lax.ppermute(lax.slice_in_dim(block, 0, width, axis=dim), axis, backward)  57.6 us
    dot_general x48, matrix products, transform(): jnp.einsum('ij,bjq->biq', left_table, partial_value, preferred_element_ty...  54.9 us
    dynamic_update_slice x8, local copies, waits for them, and re-layouts, visit_slot(): gradient = lax.dynamic_update_slice(gradient, current + slice_grads, corner)  34.8 us
    another operation x1, loops' own time, on_device(): lax.scan(visit_slot, initial, (incoming, local_row, local_col, slot_live....  33.2 us
    ppermute x4, starting transfers between devices, extended_2(): lax.ppermute(lax.slice_in_dim(block, block.shape[dim] - width, None, axis...  30.5 us
    all_gather x1, waiting for transfers between devices, on_device(): summed = jnp.sum(lax.all_gather(probe_grad, ('ty', 'tx')), axis=0)  29.7 us
    dynamic_slice x40, local copies, waits for them, and re-layouts, on_device(): lax.scan(visit_slot, initial, (incoming, local_row, local_col, slot_live....  21.2 us
    another operation x24, other arithmetic, complex_product(): jnp.stack([former_re * latter_re - former_im * latter_im, former_re * lat...  16.5 us
  transfers between devices with their start and end apart: 10, of which 5 were waited for; matrix products, arithmetic and copies ran while one was open for 12% of the time, Pallas kernels for 0%

profile of v1, /device:TPU:0, one launch (start us, length us, event | category | flops | bytes accessed | tf_op | source)
XLA Modules:
  0.0 457.9 jit_solution(11382662136670310907)
XLA Ops:
  9.8 5.6 %collective-permute-start = (f32[2,2,64,512]{3,2,1,0:T(8,128)S(1)}, f32[2,2,64,512]{3,2,1,0:T(8,128)S(1)}, u32[]{:S(2)}, u32[]{:S(2)}) collective-permute-start(f32[2,2,64,512]{3,2,1,0:T(8,128)S(1)} %get-tuple-element.545), channel_id=1, source_target_pairs={{0,8},{8,16},{16,24},{1,9},{9,17},{17,25},{2,10},{10,18},{18,26},{... | collective-permute-start | bytes 1572872 | tf_op jit(solution)/shard_map/ppermute | solution.py:16
  18.6 4.3 all-to-all-start
  22.9 5.2 %copy.122 = f32[2,2,512,512]{2,3,1,0:T(8,128)} copy(f32[2,2,512,512]{3,2,1,0:T(8,128)} %param.7) | data formatting | bytes 8388608 | tf_op args[0]
  29.7 3.1 pad_maximum_fusion.4
  34.1 3.9 collective-permute-start.2
  41.1 6.1 %pad_maximum_fusion = f32[2,2,640,640]{2,3,1,0:T(8,128)} fusion(f32[2,2,640,64]{2,3,1,0:T(8,128)} %collective-permute-done.3, f32[2,2,64,512]{2,3,1,0:T(8,128)S(1)} %copy.108, f32[2,2,512,512]{2,3,1,0:T(8,128)} %copy.122, f32[2,2,64,512]{2,3,1,0:T(8,128)} %copy-done.11, f32[2,2,640,64]{2,3,1,0:T(8,128)} %collective-permute-done.2), kind=kLoop, calls=%fused_computation.110 | loop fusion | flops 6553600 | bytes 13107200 | tf_op jit(solution)/shard_map/concatenate | solution.py:20
  47.1 3.1 broadcast_in_dim.8
  50.3 233.9 %while.18 = (s32[]{:T(128)}, f32[2,2,640,640]{2,3,1,0:T(8,128)}, f32[4,2,128,128]{3,2,0,1:T(8,128)S(1)}, s32[8]{0:T(128)S(1)}, s32[8]{0:T(128)S(1)}, /*index=5*/...) while((s32[]{:T(128)}, f32[2,2,640,640]{2,3,1,0:T(8,128)}, ...), condition=%wide.region_8.9_spmd.clone.clone.clone.clone, body=%wide.region_4.8_spmd.clone.clone.clone.clone.sunk | while | flops 815677440 | bytes 33915896 | solution.py:187
  63.7 1.5 fusion.155
  75.1 4.3 dynamic_update_slice.10
  92.9 1.5 fusion.155
  104.4 4.2 dynamic_update_slice.10
  133.5 4.4 dynamic_update_slice.10
  162.7 4.4 dynamic_update_slice.10
  192.0 4.4 dynamic_update_slice.10
  221.2 4.3 dynamic_update_slice.10
  250.5 4.4 dynamic_update_slice.10
  279.7 4.4 dynamic_update_slice.10
  285.0 8.2 %copy.116 = f32[2,2,640,640]{3,2,1,0:T(8,128)} copy(f32[2,2,640,640]{2,3,1,0:T(8,128)} %get-tuple-element.206) | data formatting | bytes 13107200 | tf_op jit(solution)/shard_map/while | solution.py:187
  294.3 2.4 collective-permute-start.4
  296.7 8.0 %collective-permute-done.4 = f32[2,2,64,640]{3,2,1,0:T(8,128)S(1)} collective-permute-done((f32[2,2,64,640]{3,2,1,0:T(8,128)S(1)}, f32[2,2,64,640]{3,2,1,0:T(8,128)S(1)}, u32[]{:S(2)}, u32[]{:S(2)}) %collective-permute-start.4) | collective-permute-done | bytes 655392 | tf_op jit(solution)/shard_map/ppermute | solution.py:16
  304.8 1.5 slice_add_fusion.7
  307.8 4.3 slice.281
  312.4 15.2 %collective-permute-done.5 = f32[2,2,64,640]{3,2,1,0:T(8,128)S(1)} collective-permute-done((f32[2,2,64,640]{3,2,1,0:T(8,128)S(1)}, f32[2,2,64,640]{3,2,1,0:T(8,128)S(1)}, u32[]{:S(2)}, u32[]{:S(2)}) %collective-permute-start.5) | collective-permute-done | bytes 655392 | tf_op jit(solution)/shard_map/ppermute | solution.py:19
  330.6 18.5 %collective-permute-start.6 = (f32[2,2,512,64]{2,3,1,0:T(8,128)S(1)}, f32[2,2,512,64]{2,3,1,0:T(8,128)S(1)}, u32[]{:S(2)}, u32[]{:S(2)}) collective-permute-start(f32[2,2,512,64]{2,3,1,0:T(8,128)S(1)} %pad_maximum_fusion.6), channel_id=1, source_target_pairs={{0,1},{1,2},{2,3},{3,4},{4,5},{5,6},{6,7},{8,9},{9,10},{10,11},{11... | collective-permute-start | bytes 1572872 | tf_op jit(solution)/shard_map/ppermute | solution.py:16
  349.1 1.5 collective-permute-done.6
  355.5 3.9 pad_maximum_fusion.1
  359.8 42.4 %collective-permute-done.7 = f32[2,2,512,64]{2,3,1,0:T(8,128)} collective-permute-done((f32[2,2,512,64]{2,3,1,0:T(8,128)}, f32[2,2,512,64]{2,3,1,0:T(8,128)}, u32[]{:S(2)}, u32[]{:S(2)}) %collective-permute-start.7) | collective-permute-done | bytes 524320 | tf_op jit(solution)/shard_map/ppermute | solution.py:19
  403.5 3.0 fusion.85
  406.5 5.2 %copy.125 = f32[2,2,512,512]{3,2,1,0:T(8,128)} copy(f32[2,2,512,512]{2,3,1,0:T(8,128)} %fusion.85) | data formatting | bytes 8388608
  411.7 29.7 %all-gather.3.cloned.1.call-done = f32[128,2,128,128]{3,2,0,1:T(8,128)} async-done(((f32[4,2,128,128]{3,2,0,1:T(8,128)}), f32[128,2,128,128]{3,2,0,1:T(8,128)}) %all-gather.3.cloned.1.call-update) | async-done | bytes 16777232 | tf_op jit(solution)/shard_map/all_gather | solution.py:210
  441.3 7.0 %reduce_sum.95 = f32[4,2,128,128]{3,2,0,1:T(8,128)S(1)} reduce(f32[32,4,2,128,128]{4,3,1,0,2:T(8,128)} %bitcast.205, f32[]{:T(128)} %constant.97.clone.1), dimensions={0}, to_apply=%region_10.11 | reduce | flops 4063232 | bytes 17301508 | tf_op jit(solution)/shard_map/reduce_sum | solution.py:210
  (463 shorter events, 189.1 us)
Async XLA Ops:
  7.2 10.4 %copy-start = (bf16[8,128,128]{2,1,0:T(8,128)(2,1)S(1)}, bf16[8,128,128]{2,1,0:T(8,128)(2,1)}, u32[]{:S(2)}) copy-start(bf16[8,128,128]{2,1,0:T(8,128)(2,1)} %param.9) | copy-start | bytes 786436
  8.5 20.4 %collective-permute-start.1 = (f32[2,2,64,512]{3,2,1,0:T(8,128)S(1)}, f32[2,2,64,512]{3,2,1,0:T(8,128)S(1)}, u32[]{:S(2)}, u32[]{:S(2)}) collective-permute-start(f32[2,2,64,512]{3,2,1,0:T(8,128)S(1)} %get-tuple-element.546), channel_id=1, source_target_pairs={{8,0},{16,8},{24,16},{9,1},{17,9},{25,17},{10,2},{18,10},{26,18},{... | collective-permute-start | bytes 1572872 | tf_op jit(solution)/shard_map/ppermute | solution.py:19
  9.8 19.5 %collective-permute-start = (f32[2,2,64,512]{3,2,1,0:T(8,128)S(1)}, f32[2,2,64,512]{3,2,1,0:T(8,128)S(1)}, u32[]{:S(2)}, u32[]{:S(2)}) collective-permute-start(f32[2,2,64,512]{3,2,1,0:T(8,128)S(1)} %get-tuple-element.545), channel_id=1, source_target_pairs={{0,8},{8,16},{16,24},{1,9},{9,17},{17,25},{2,10},{10,18},{18,26},{... | collective-permute-start | bytes 1572872 | tf_op jit(solution)/shard_map/ppermute | solution.py:16
  18.6 28.6 %all-to-all-start = ((bf16[8,128,128]{2,1,0:T(8,128)(2,1)}), bf16[8,128,128]{2,1,0:T(8,128)(2,1)}, u32[]{:S(2)}, u32[]{:S(2)}) async-start(bf16[8,128,128]{2,1,0:T(8,128)(2,1)} %copy.110), calls=%async_computation | async-start | bytes 524288 | tf_op jit(solution)/shard_map/all_to_all | solution.py:154
  22.9 418.5 %all-gather.3.cloned.1.call-start = ((), (), s32[]{:S(2)}) async-start(), calls=%async_computation.1 | async-start | bytes 17301504 | tf_op jit(solution)/shard_map/all_gather | solution.py:210
  29.7 9.0 %copy-start.13 = (f32[4,2,128,128]{3,2,1,0:T(8,128)S(1)}, f32[4,2,128,128]{3,2,1,0:T(8,128)}, u32[]{:S(2)}) copy-start(f32[4,2,128,128]{3,2,1,0:T(8,128)} %param.8) | copy-start | bytes 1572868
  32.8 8.2 %collective-permute-start.3 = (f32[2,2,640,64]{2,3,1,0:T(8,128)}, f32[2,2,640,64]{2,3,1,0:T(8,128)}, u32[]{:S(2)}, u32[]{:S(2)}) collective-permute-start(f32[2,2,640,64]{2,3,1,0:T(8,128)} %get-tuple-element.544), channel_id=1, source_target_pairs={{1,0},{2,1},{3,2},{4,3},{5,4},{6,5},{7,6},{9,8},{10,9},{11,10},{12... | collective-permute-start | bytes 1966088 | tf_op jit(solution)/shard_map/ppermute | solution.py:19
  34.1 6.9 %collective-permute-start.2 = (f32[2,2,640,64]{2,3,1,0:T(8,128)}, f32[2,2,640,64]{2,3,1,0:T(8,128)}, u32[]{:S(2)}, u32[]{:S(2)}) collective-permute-start(f32[2,2,640,64]{2,3,1,0:T(8,128)} %get-tuple-element.543), channel_id=1, source_target_pairs={{0,1},{1,2},{2,3},{3,4},{4,5},{5,6},{6,7},{8,9},{9,10},{10,11},{11... | collective-permute-start | bytes 1966088 | tf_op jit(solution)/shard_map/ppermute | solution.py:16
  50.3 10.7 %copy-start.6 = (bf16[256,128]{1,0:T(8,128)(2,1)}, bf16[256,128]{1,0:T(8,128)(2,1)S(1)}, u32[]{:S(2)}) copy-start(bf16[256,128]{1,0:T(8,128)(2,1)S(1)} %get-tuple-element.766) | copy-start | bytes 196612 | tf_op jit(solution)/shard_map/while
  79.5 10.7 %copy-start.6 = (bf16[256,128]{1,0:T(8,128)(2,1)}, bf16[256,128]{1,0:T(8,128)(2,1)S(1)}, u32[]{:S(2)}) copy-start(bf16[256,128]{1,0:T(8,128)(2,1)S(1)} %get-tuple-element.766) | copy-start | bytes 196612 | tf_op jit(solution)/shard_map/while
  108.6 10.7 %copy-start.6 = (bf16[256,128]{1,0:T(8,128)(2,1)}, bf16[256,128]{1,0:T(8,128)(2,1)S(1)}, u32[]{:S(2)}) copy-start(bf16[256,128]{1,0:T(8,128)(2,1)S(1)} %get-tuple-element.766) | copy-start | bytes 196612 | tf_op jit(solution)/shard_map/while
  130.8 7.1 %copy-start.7 = (bf16[256,128]{1,0:T(8,128)(2,1)S(1)}, bf16[256,128]{1,0:T(8,128)(2,1)}, u32[]{:S(2)}) copy-start(bf16[256,128]{1,0:T(8,128)(2,1)} %copy-done.6) | copy-start | bytes 196612 | tf_op jit(solution)/shard_map/while
  137.9 10.7 %copy-start.6 = (bf16[256,128]{1,0:T(8,128)(2,1)}, bf16[256,128]{1,0:T(8,128)(2,1)S(1)}, u32[]{:S(2)}) copy-start(bf16[256,128]{1,0:T(8,128)(2,1)S(1)} %get-tuple-element.766) | copy-start | bytes 196612 | tf_op jit(solution)/shard_map/while
  160.0 7.1 %copy-start.7 = (bf16[256,128]{1,0:T(8,128)(2,1)S(1)}, bf16[256,128]{1,0:T(8,128)(2,1)}, u32[]{:S(2)}) copy-start(bf16[256,128]{1,0:T(8,128)(2,1)} %copy-done.6) | copy-start | bytes 196612 | tf_op jit(solution)/shard_map/while
  167.1 10.7 %copy-start.6 = (bf16[256,128]{1,0:T(8,128)(2,1)}, bf16[256,128]{1,0:T(8,128)(2,1)S(1)}, u32[]{:S(2)}) copy-start(bf16[256,128]{1,0:T(8,128)(2,1)S(1)} %get-tuple-element.766) | copy-start | bytes 196612 | tf_op jit(solution)/shard_map/while
  189.3 7.1 %copy-start.7 = (bf16[256,128]{1,0:T(8,128)(2,1)S(1)}, bf16[256,128]{1,0:T(8,128)(2,1)}, u32[]{:S(2)}) copy-start(bf16[256,128]{1,0:T(8,128)(2,1)} %copy-done.6) | copy-start | bytes 196612 | tf_op jit(solution)/shard_map/while
  196.4 10.7 %copy-start.6 = (bf16[256,128]{1,0:T(8,128)(2,1)}, bf16[256,128]{1,0:T(8,128)(2,1)S(1)}, u32[]{:S(2)}) copy-start(bf16[256,128]{1,0:T(8,128)(2,1)S(1)} %get-tuple-element.766) | copy-start | bytes 196612 | tf_op jit(solution)/shard_map/while
  225.6 10.7 %copy-start.6 = (bf16[256,128]{1,0:T(8,128)(2,1)}, bf16[256,128]{1,0:T(8,128)(2,1)S(1)}, u32[]{:S(2)}) copy-start(bf16[256,128]{1,0:T(8,128)(2,1)S(1)} %get-tuple-element.766) | copy-start | bytes 196612 | tf_op jit(solution)/shard_map/while
  247.8 7.1 %copy-start.7 = (bf16[256,128]{1,0:T(8,128)(2,1)S(1)}, bf16[256,128]{1,0:T(8,128)(2,1)}, u32[]{:S(2)}) copy-start(bf16[256,128]{1,0:T(8,128)(2,1)} %copy-done.6) | copy-start | bytes 196612 | tf_op jit(solution)/shard_map/while
  254.8 10.7 %copy-start.6 = (bf16[256,128]{1,0:T(8,128)(2,1)}, bf16[256,128]{1,0:T(8,128)(2,1)S(1)}, u32[]{:S(2)}) copy-start(bf16[256,128]{1,0:T(8,128)(2,1)S(1)} %get-tuple-element.766) | copy-start | bytes 196612 | tf_op jit(solution)/shard_map/while
  277.0 7.1 %copy-start.7 = (bf16[256,128]{1,0:T(8,128)(2,1)S(1)}, bf16[256,128]{1,0:T(8,128)(2,1)}, u32[]{:S(2)}) copy-start(bf16[256,128]{1,0:T(8,128)(2,1)} %copy-done.6) | copy-start | bytes 196612 | tf_op jit(solution)/shard_map/while
  294.3 10.5 %collective-permute-start.4 = (f32[2,2,64,640]{3,2,1,0:T(8,128)S(1)}, f32[2,2,64,640]{3,2,1,0:T(8,128)S(1)}, u32[]{:S(2)}, u32[]{:S(2)}) collective-permute-start(f32[2,2,64,640]{3,2,1,0:T(8,128)S(1)} %slice.455), channel_id=1, source_target_pairs={{0,8},{8,16},{16,24},{1,9},{9,17},{17,25},{2,10},{10,18},{18,26},{... | collective-permute-start | bytes 1966088 | tf_op jit(solution)/shard_map/ppermute | solution.py:16
  306.3 21.3 %collective-permute-start.5 = (f32[2,2,64,640]{3,2,1,0:T(8,128)S(1)}, f32[2,2,64,640]{3,2,1,0:T(8,128)S(1)}, u32[]{:S(2)}, u32[]{:S(2)}) collective-permute-start(f32[2,2,64,640]{3,2,1,0:T(8,128)S(1)} %get-tuple-element.542), channel_id=1, source_target_pairs={{8,0},{16,8},{24,16},{9,1},{17,9},{25,17},{10,2},{18,10},{26,18},{... | collective-permute-start | bytes 1966088 | tf_op jit(solution)/shard_map/ppermute | solution.py:19
  329.2 21.4 %copy-start.2 = (f32[2,2,384,640]{2,3,1,0:T(8,128)S(1)}, f32[2,2,384,640]{2,3,1,0:T(8,128)}, u32[]{:S(2)}) copy-start(f32[2,2,384,640]{2,3,1,0:T(8,128)} %slice.281) | copy-start | bytes 11796484
  330.6 22.7 %copy-start.14 = (f32[4,2,128,128]{3,2,1,0:T(8,128)S(1)}, f32[4,2,128,128]{3,2,1,0:T(8,128)}, u32[]{:S(2)}) copy-start(f32[4,2,128,128]{3,2,1,0:T(8,128)} %param.8) | copy-start | bytes 1572868
  330.6 20.0 %collective-permute-start.6 = (f32[2,2,512,64]{2,3,1,0:T(8,128)S(1)}, f32[2,2,512,64]{2,3,1,0:T(8,128)S(1)}, u32[]{:S(2)}, u32[]{:S(2)}) collective-permute-start(f32[2,2,512,64]{2,3,1,0:T(8,128)S(1)} %pad_maximum_fusion.6), channel_id=1, source_target_pairs={{0,1},{1,2},{2,3},{3,4},{4,5},{5,6},{6,7},{8,9},{9,10},{10,11},{11... | collective-permute-start | bytes 1572872 | tf_op jit(solution)/shard_map/ppermute | solution.py:16
  352.0 50.2 %collective-permute-start.7 = (f32[2,2,512,64]{2,3,1,0:T(8,128)}, f32[2,2,512,64]{2,3,1,0:T(8,128)}, u32[]{:S(2)}, u32[]{:S(2)}) collective-permute-start(f32[2,2,512,64]{2,3,1,0:T(8,128)} %get-tuple-element.540), channel_id=1, source_target_pairs={{1,0},{2,1},{3,2},{4,3},{5,4},{6,5},{7,6},{9,8},{10,9},{11,10},{12... | collective-permute-start | bytes 1572872 | tf_op jit(solution)/shard_map/ppermute | solution.py:19
  359.4 42.8 %copy-start.3 = (f32[2,2,384,640]{2,3,1,0:T(8,128)S(1)}, f32[2,2,384,640]{2,3,1,0:T(8,128)}, u32[]{:S(2)}) copy-start(f32[2,2,384,640]{2,3,1,0:T(8,128)} %slice.281) | copy-start | bytes 11796484
  359.7 43.8 %copy-start.4 = (f32[2,2,512,512]{2,3,1,0:T(8,128)S(1)}, f32[2,2,512,512]{2,3,1,0:T(8,128)}, u32[]{:S(2)}) copy-start(f32[2,2,512,512]{2,3,1,0:T(8,128)} %copy.122) | copy-start | bytes 12582916
  359.7 43.8 %copy-start.15 = (f32[2,2,512,64]{2,3,1,0:T(8,128)S(1)}, f32[2,2,512,64]{2,3,1,0:T(8,128)}, u32[]{:S(2)}) copy-start(f32[2,2,512,64]{2,3,1,0:T(8,128)} %get-tuple-element.539) | copy-start | bytes 1572868
  441.3 8.6 %copy-start.16 = (f32[4,2,128,128]{2,3,0,1:T(8,128)S(1)}, f32[4,2,128,128]{2,3,0,1:T(8,128)}, u32[]{:S(2)}) copy-start(f32[4,2,128,128]{2,3,0,1:T(8,128)} %copy.124) | copy-start | bytes 1572868
  441.3 9.7 %copy-start.1 = (bf16[8,128,128]{2,1,0:T(8,128)(2,1)S(1)}, bf16[8,128,128]{2,1,0:T(8,128)(2,1)}, u32[]{:S(2)}) copy-start(bf16[8,128,128]{2,1,0:T(8,128)(2,1)} %param.9) | copy-start | bytes 786436
  (37 other events, 132.3 us)
Sparse Core Ops, SparseCore 0:
  285.1 156.2 all-gather.2
